TPU v7x, 256 devices: a whole 4x4x8 slice. The times are simulated.
256 devices in a mesh: tensor: 64 (over x_hi, y, z), dp: 4 (over x_lo, core).
Axes of the slice: x: 4 (x_hi: 2, x_lo: 2; x = x_hi * 2 + x_lo), y: 4, z: 8, core: 2. Of those that a mesh axis runs over, the one named last changes fastest.
Arguments:
- base_weight: bfloat16 [2, 2, 4096, 14336], P(None, None, 'tensor', 'dp'), may hold values from -0.25 to 0.25
- adapter_left: bfloat16 [2, 2, 4096, 16], P(None, None, 'tensor'), may hold values from -0.059814453 to 0.059814453
- adapter_right: bfloat16 [2, 2, 16, 14336], P(None, None, None, 'dp'), may hold values from -1.5 to 1.5
- magnitude: bfloat16 [2, 2, 14336], P(None, None, 'dp'), may hold values from 16 to 256
Outputs:
- merged_weight: bfloat16 [2, 2, 14336, 4096], P(None, None, 'tensor')
All inputs are finite; a program needn't handle non-finite values.
Results may differ from a plain program's by a relative error of at most 0.0004.
Values may be sent and summed in bfloat16 or wider, within the bound.
A program may use at most 128 MiB of HBM per device.

v0:
```python
import jax
import jax.numpy as jnp
from jax import lax
from jax.sharding import PartitionSpec as P


def cut_along(array, dim, length):
    before, after = (array.shape[:dim], array.shape[dim + 1 :])
    return jnp.moveaxis(array.reshape(*before, length, -1, *after), dim, 0)


def edges_of(length, count):
    lap = length // count
    if lap >= 8:
        lap -= lap % 8
    return [lap * k for k in range(1, count)]


def laid_out(tiles, dim):
    tiles = jnp.moveaxis(tiles, 0, dim)
    shape = tiles.shape
    return tiles.reshape(*shape[:dim], shape[dim] * shape[dim + 1], *shape[dim + 2 :])


def exchange_in_pieces(array, axis, pieces, split_dim, concat_dim):
    tiles = cut_along(array, split_dim, lax.axis_size(axis))
    split_at = max(range(1, max(2, tiles.ndim - 1)), key=lambda d: tiles.shape[d])
    finished = []
    for piece in jnp.split(tiles, edges_of(tiles.shape[split_at], pieces), axis=split_at):
        if piece.size:
            finished.append(lax.all_to_all(piece, axis, split_axis=0, concat_axis=0, tiled=True))
    return laid_out(jnp.concatenate(finished, axis=split_at), concat_dim)


def copy_for_each(array, axis):
    copies = jnp.broadcast_to(array, (lax.axis_size(axis), *array.shape))
    return lax.all_to_all(copies, axis, split_axis=0, concat_axis=0, tiled=True)


def collect(array, axis, dim):
    tiles = copy_for_each(array, axis)
    return laid_out(tiles, dim)


def turned_gather(arrays, axis, dims):
    turned = [jnp.moveaxis(a, dim, 0) for a, dim in zip(arrays, dims)]
    widths = [t[0].size for t in turned]
    both = jnp.concatenate([t.reshape(-1, w) for t, w in zip(turned, widths)], axis=1)
    whole = lax.all_gather(both, axis, axis=0, tiled=True)
    tiles = jnp.split(whole, [sum(widths[:k]) for k in range(1, len(widths))], axis=1)
    return tuple(
        (
            jnp.moveaxis(b.reshape(-1, *t.shape[1:]), 0, dim)
            for b, t, dim in zip(tiles, turned, dims)
        )
    )


def regroup(weight_slab):
    experts, projections, row_count, col_count = weight_slab.shape
    tensor_count = lax.axis_size("tensor")
    replica_count = lax.axis_size("dp")
    serve_cols = col_count * replica_count // tensor_count
    quartered = lax.all_to_all(weight_slab, "dp", split_axis=2, concat_axis=3, tiled=True)
    grouped = exchange_in_pieces(quartered, "tensor", 2, 3, 2)
    collected = lax.all_gather(grouped, "dp", axis=2, tiled=True)
    pieces_view = collected.reshape(
        experts, projections, replica_count, tensor_count, row_count // replica_count, serve_cols
    )
    return pieces_view.transpose(0, 1, 5, 3, 2, 4).reshape(
        experts, projections, serve_cols, tensor_count * row_count
    )


def shards(base_weight, adapter_left, adapter_right, magnitude):
    tensor_count = lax.axis_size("tensor")
    replica_count = lax.axis_size("dp")
    col_count = base_weight.shape[3]
    serve_cols = col_count * replica_count // tensor_count
    arrived = regroup(base_weight)
    left_full = collect(adapter_left, "tensor", 2)
    right_all, magnitude_all = turned_gather((adapter_right, magnitude), "dp", (3, 2))
    col_start = lax.axis_index("tensor") * serve_cols
    right_cols = lax.dynamic_slice_in_dim(right_all, col_start, serve_cols, 3)
    magnitude_cols = lax.dynamic_slice_in_dim(magnitude_all, col_start, serve_cols, 2)
    merged = arrived.astype(jnp.float32) + jnp.einsum(
        "xyrf,xyir->xyfi", right_cols, left_full, preferred_element_type=jnp.float32
    )
    squares = jnp.sum(merged * merged, axis=3)
    scaling = magnitude_cols.astype(jnp.float32) / jnp.sqrt(squares + 1e-06)
    return (merged * scaling[:, :, :, None]).astype(jnp.bfloat16)


def solution(mesh):
    in_specs = (
        P(None, None, "tensor", "dp"),
        P(None, None, "tensor", None),
        P(None, None, None, "dp"),
        P(None, None, "dp"),
    )
    out_specs = P(None, None, "tensor", None)
    return jax.shard_map(shards, mesh=mesh, in_specs=in_specs, out_specs=out_specs, check_vma=False)
```

profile of v0, /device:TPU:1, one launch (start us, length us, event | category | flops | bytes accessed | tf_op | source)
XLA Modules:
  0.0 277.2 jit_solution(4250908606678984291)
XLA Ops:
  6.5 3.4 %copy.9 = bf16[2,2,64,3584]{3,1,0,2:T(2,128)(2,1)S(1)} copy(bf16[2,2,64,3584]{3,2,1,0:T(8,128)(2,1)} %param.4) | data formatting | bytes 3670016 | tf_op args[0]
  9.9 27.5 %all_to_all.30 = bf16[2,2,64,3584]{3,1,0,2:T(2,128)(2,1)S(1)} all-to-all(bf16[2,2,64,3584]{3,1,0,2:T(2,128)(2,1)S(1)} %copy.9), channel_id=1, replica_groups=mesh['tensor'=64,'dp'=4] {'dp'}, dimensions={2} | all-to-all | bytes 3670016 | tf_op jit(solution)/shard_map/all_to_all | solution.py:64
  37.4 2.6 copy.18
  40.1 4.4 %reshape.29 = bf16[2,2,16,64,224]{4,3,2,1,0:T(8,128)(2,1)S(1)} reshape(bf16[2,2,16,4,3584]{4,3,2,1,0:T(4,128)(2,1)} %bitcast.45) | data formatting | bytes 3670016 | tf_op jit(solution)/shard_map/reshape | solution.py:9
  44.5 0.2 fusion.3
  44.7 1.6 copy.12
  46.2 12.6 %all-to-all-start.2 = ((bf16[64,2,2,8,224]{4,3,2,1,0:T(8,128)(2,1)}), bf16[64,2,2,8,224]{4,3,2,1,0:T(8,128)(2,1)S(1)}, u32[]{:S(2)}, u32[]{:S(2)}) async-start(bf16[64,2,2,8,224]{4,3,2,1,0:T(8,128)(2,1)} %copy.12), calls=%async_computation.2 | async-start | bytes 2097152 | tf_op jit(solution)/shard_map/all_to_all | solution.py:31
  58.8 0.0 all-gather.5.cloned.1.call-start
  58.9 0.9 pad_maximum_fusion
  59.8 0.0 all-gather.3.cloned.1.call-start
  59.8 0.6 copy.11
  60.4 26.0 %all-to-all-done.2 = bf16[64,2,2,8,224]{4,3,2,1,0:T(8,128)(2,1)S(1)} async-done(((bf16[64,2,2,8,224]{4,3,2,1,0:T(8,128)(2,1)}), bf16[64,2,2,8,224]{4,3,2,1,0:T(8,128)(2,1)S(1)}, u32[]{:S(2)}, u32[]{:S(2)}) %all-to-all-start.2) | async-done | bytes 917536 | tf_op jit(solution)/shard_map/all_to_all | solution.py:31
  86.4 34.1 %all_to_all.31 = bf16[64,2,2,8,224]{4,3,2,1,0:T(8,128)(2,1)S(1)} all-to-all(bf16[64,2,2,8,224]{4,3,2,1,0:T(8,128)(2,1)S(1)} %copy.11), channel_id=1, replica_groups=mesh['tensor'=64,'dp'=4] {'tensor'}, dimensions={0} | all-to-all | bytes 1835008 | tf_op jit(solution)/shard_map/all_to_all | solution.py:31
  120.5 0.6 maximum_bitcast_fusion
  121.1 1.5 copy.13
  122.7 0.2 broadcast_bitcast_fusion
  122.9 1.6 reshape.38
  124.5 8.6 %all-to-all-start.3 = ((bf16[64,2,2048]{2,1,0:T(2,128)(2,1)}), bf16[64,2,2048]{2,1,0:T(2,128)(2,1)S(1)}, u32[]{:S(2)}, u32[]{:S(2)}) async-start(bf16[64,2,2048]{2,1,0:T(2,128)(2,1)} %reshape.38), calls=%async_computation.3 | async-start | bytes 1048576 | tf_op jit(solution)/shard_map/all_to_all | solution.py:37
  133.1 15.9 %all-to-all-done.3 = bf16[64,2,2048]{2,1,0:T(2,128)(2,1)S(1)} async-done(((bf16[64,2,2048]{2,1,0:T(2,128)(2,1)}), bf16[64,2,2048]{2,1,0:T(2,128)(2,1)S(1)}, u32[]{:S(2)}, u32[]{:S(2)}) %all-to-all-start.3) | async-done | bytes 524320 | tf_op jit(solution)/shard_map/all_to_all | solution.py:37
  149.0 0.7 reshape.39
  149.6 0.1 bitcast_bitcast_fusion
  149.8 0.7 copy.15
  150.5 0.8 reshape.34
  151.3 1.0 split.19
  152.3 0.1 reshape.35
  152.4 57.5 %all-gather.3.cloned.1.call-done = bf16[2,2,4096,224]{3,2,1,0:T(8,128)(2,1)} async-done(((bf16[2,2,1024,224]{3,2,1,0:T(8,128)(2,1)}), bf16[2,2,4096,224]{3,2,1,0:T(8,128)(2,1)}) %all-gather.3.cloned.1.call-update) | async-done | bytes 7340048 | tf_op jit(solution)/shard_map/all_gather | solution.py:66
  209.9 11.4 %convert_bitcast_fusion = f32[2,2,224,64,4,16]{2,5,3,4,1,0:T(8,128)} fusion(bf16[2,2,4,64,16,224]{5,4,3,2,1,0:T(8,128)(2,1)} %bitcast.41), kind=kLoop, calls=%fused_computation | loop fusion | flops 3670016 | bytes 22020096 | tf_op jit(solution)/shard_map/convert_element_type | solution.py:86
  221.3 11.9 %copy.14 = f32[2,2,224,64,4,16]{2,5,4,3,1,0:T(8,128)} copy(f32[2,2,224,64,4,16]{2,5,3,4,1,0:T(8,128)} %convert_bitcast_fusion) | data formatting | bytes 29360128 | tf_op jit(solution)/shard_map/convert_element_type | solution.py:86
  233.2 17.0 %copy.16 = f32[2,2,224,4096]{3,2,1,0:T(8,128)} copy(f32[2,2,224,4096]{2,3,1,0:T(8,128)} %bitcast.40) | data formatting | bytes 29360128 | tf_op jit(solution)/shard_map/convert_element_type | solution.py:86
  250.2 9.5 %multiply_reduce_fusion = (f32[2,2,224]{2,1,0:T(2,128)S(1)}, f32[2,2,224,4096]{3,2,1,0:T(8,128)}) fusion(f32[2,2,224,4096]{3,2,1,0:T(8,128)} %copy.16, bf16[2,2,4096,16]{2,3,1,0:T(8,128)(2,1)S(1)} %reshape.34, bf16[14336,2,2,16]{0,3,2,1:T(8,128)(2,1)S(1)} %bitcast.46, s32[]{:T(128)S(6)} %select_n.4), kind=kOutput, calls=%fused_computation.2 | convolution fusion | flops 128449664 | bytes 29920772 | tf_op jit(solution)/shard_map/xyrf,xyir->xyfi/dot_general | solution.py:86
  259.7 0.1 bitcast_multiply_fusion
  259.8 10.6 %multiply_convert_fusion = bf16[2,2,224,4096]{3,2,1,0:T(8,128)(2,1)} fusion(f32[2,2,224,4096]{3,2,1,0:T(8,128)} %get-tuple-element.8, f32[2,2,224]{2,1,0:T(2,128)S(1)} %bitcast_multiply_fusion), kind=kLoop, calls=%fused_computation.1 | loop fusion | flops 7340032 | bytes 22023680 | tf_op jit(solution)/shard_map/convert_element_type | solution.py:91
  (14 shorter events, 0.1 us)
Async XLA Ops:
  6.5 116.1 %copy-start = (bf16[2,2,64,16]{2,3,1,0:T(8,128)(2,1)S(1)}, bf16[2,2,64,16]{2,3,1,0:T(8,128)(2,1)}, u32[]{:S(2)}) copy-start(bf16[2,2,64,16]{2,3,1,0:T(8,128)(2,1)} %param.5) | copy-start | bytes 24580
  44.5 14.4 %copy-start.3 = (bf16[2,2,3584]{2,1,0:T(2,128)(2,1)S(1)}, bf16[2,2,3584]{2,1,0:T(2,128)(2,1)}, u32[]{:S(2)}) copy-start(bf16[2,2,3584]{2,1,0:T(2,128)(2,1)} %param.7) | copy-start | bytes 86020
  44.7 14.2 %copy-start.2 = (bf16[2,2,16,3584]{3,2,1,0:T(8,128)(2,1)S(1)}, bf16[2,2,16,3584]{3,2,1,0:T(8,128)(2,1)}, u32[]{:S(2)}) copy-start(bf16[2,2,16,3584]{3,2,1,0:T(8,128)(2,1)} %param.6) | copy-start | bytes 1376260
  46.2 40.2 %all-to-all-start.2 = ((bf16[64,2,2,8,224]{4,3,2,1,0:T(8,128)(2,1)}), bf16[64,2,2,8,224]{4,3,2,1,0:T(8,128)(2,1)S(1)}, u32[]{:S(2)}, u32[]{:S(2)}) async-start(bf16[64,2,2,8,224]{4,3,2,1,0:T(8,128)(2,1)} %copy.12), calls=%async_computation.2 | async-start | bytes 2097152 | tf_op jit(solution)/shard_map/all_to_all | solution.py:31
  58.8 92.5 %all-gather.5.cloned.1.call-start = ((), (), s32[]{:S(2)}) async-start(), calls=%async_computation.5 | async-start | bytes 2580480 | tf_op jit(solution)/shard_map/all_gather | solution.py:49
  59.8 150.1 %all-gather.3.cloned.1.call-start = ((), (), s32[]{:S(2)}) async-start(), calls=%async_computation.4 | async-start | bytes 10485760 | tf_op jit(solution)/shard_map/all_gather | solution.py:66
  124.5 24.5 %all-to-all-start.3 = ((bf16[64,2,2048]{2,1,0:T(2,128)(2,1)}), bf16[64,2,2048]{2,1,0:T(2,128)(2,1)S(1)}, u32[]{:S(2)}, u32[]{:S(2)}) async-start(bf16[64,2,2048]{2,1,0:T(2,128)(2,1)} %reshape.38), calls=%async_computation.3 | async-start | bytes 1048576 | tf_op jit(solution)/shard_map/all_to_all | solution.py:37
  233.2 17.0 %slice-start = ((bf16[14336,68]{0,1:T(8,128)(2,1)}), bf16[14336,64]{0,1:T(8,128)(2,1)S(1)}, s32[]{:S(2)}) async-start(bf16[14336,68]{0,1:T(8,128)(2,1)} %all-gather.5.cloned.1.call-done), calls=%async_computation.6 | async-start | bytes 3670016 | tf_op jit(solution)/shard_map/split | solution.py:50
  259.8 10.6 %copy-start.1 = (bf16[2,2,64,16]{2,3,1,0:T(8,128)(2,1)S(1)}, bf16[2,2,64,16]{2,3,1,0:T(8,128)(2,1)}, u32[]{:S(2)}) copy-start(bf16[2,2,64,16]{2,3,1,0:T(8,128)(2,1)} %param.5) | copy-start | bytes 24580
Sparse Core Ops, SparseCore 0:
  61.4 38.3 all-gather.4
  122.8 87.0 all-gather.2
where the time goes:
time: 278 us; the launch traced here: 277 us
  waiting for transfers between devices  99.4 us (36%)
  blocking collectives  61.6 us (22%)
  local copies, waits for them, and re-layouts  48.4 us (17%)
  other arithmetic  23.6 us (8%)
  starting transfers between devices  21.3 us (8%)
  between operations  13.6 us (5%)
  matrix products  9.51 us (3%)
    all_gather x1, waiting for transfers between devices, regroup(): collected = lax.all_gather(grouped, 'dp', axis=2, tiled=True)  57.5 us
    all_to_all x1, blocking collectives, exchange_in_pieces(): lax.all_to_all(piece, axis, split_axis=0, concat_axis=0, tiled=True)  34.1 us
    convert_element_type x2, local copies, waits for them, and re-layouts, shards(): arrived.astype(jnp.float32)  28.9 us
    all_to_all x1, blocking collectives, regroup(): lax.all_to_all(weight_slab, 'dp', split_axis=2, concat_axis=3, tiled=True)  27.5 us
    all_to_all x1, waiting for transfers between devices, exchange_in_pieces(): lax.all_to_all(piece, axis, split_axis=0, concat_axis=0, tiled=True)  26 us
    all_to_all x1, waiting for transfers between devices, copy_for_each(): return lax.all_to_all(copies, axis, split_axis=0, concat_axis=0, tiled=True)  15.9 us
    all_to_all x1, starting transfers between devices, exchange_in_pieces(): lax.all_to_all(piece, axis, split_axis=0, concat_axis=0, tiled=True)  12.6 us
    convert_element_type x1, other arithmetic, shards(): arrived.astype(jnp.float32)  11.4 us
  transfers between devices with their start and end apart: 4, of which 3 were waited for; matrix products, arithmetic and copies ran while one was open for 3% of the time, Pallas kernels for 0%

commit v1 on v0

--- a/solution.py
+++ b/solution.py
@@ -63,7 +63,10 @@
     serve_cols = col_count * replica_count // tensor_count
     quartered = lax.all_to_all(weight_slab, "dp", split_axis=2, concat_axis=3, tiled=True)
     grouped = exchange_in_pieces(quartered, "tensor", 2, 3, 2)
-    collected = lax.all_gather(grouped, "dp", axis=2, tiled=True)
+    devices = lax.axis_size("dp")
+    blocks = jnp.stack([grouped for _ in range(devices)])
+    blocks = lax.all_to_all(blocks, "dp", split_axis=0, concat_axis=0)
+    collected = jnp.concatenate(blocks, axis=2)
     pieces_view = collected.reshape(
         experts, projections, replica_count, tensor_count, row_count // replica_count, serve_cols
     )

time: 278 us -> 342 us (1.23)
  waiting for transfers between devices: 99.4 us -> 155 us
  blocking collectives: 61.6 us -> 27.5 us
  local copies, waits for them, and re-layouts: 48.4 us -> 73.4 us
  starting transfers between devices: 21.3 us -> 39.8 us
    all_gather x1 -> x0, waiting for transfers between devices: 57.5 us -> none  [regroup(): collected = lax.all_gather(grouped, 'dp', axis=2, tiled=True)]
    all_to_all x0 -> x1, waiting for transfers between devices: none -> 50.7 us  [regroup(): blocks = lax.all_to_all(blocks, 'dp', split_axis=0, concat_axis=0)]
    all_gather x1, waiting for transfers between devices: 0.02 us -> 40.9 us  [turned_gather(): whole = lax.all_gather(both, axis, axis=0, tiled=True)]
    all_to_all x1 -> x0, blocking collectives: 34.1 us -> none  [exchange_in_pieces(): lax.all_to_all(piece, axis, split_axis=0, concat_axis=0, tiled=True)]
    all_to_all x1 -> x2, waiting for transfers between devices: 26 us -> 50.6 us  [exchange_in_pieces(): lax.all_to_all(piece, axis, split_axis=0, concat_axis=0, tiled=True)]
    convert_element_type x2 -> x3, local copies, waits for them, and re-layouts: 28.9 us -> 44.7 us  [shards(): arrived.astype(jnp.float32)]
    all_to_all x0 -> x1, starting transfers between devices: none -> 10.5 us  [regroup(): blocks = lax.all_to_all(blocks, 'dp', split_axis=0, concat_axis=0)]
    another operation x0 -> x2, local copies, waits for them, and re-layouts: none -> 7.98 us  [regroup(): blocks = jnp.stack([grouped for _ in range(devices)])]
  transfers between devices with their start and end apart: 4 -> 5, of which waited for: 3 -> 5; matrix products, arithmetic and copies ran while one was open for 3% -> 4% of each run, Pallas kernels for 0% -> 0%
where the time goes in v1:
time: 342 us; the launch traced here: 341 us
  waiting for transfers between devices  155 us (45%)
  local copies, waits for them, and re-layouts  73.4 us (21%)
  starting transfers between devices  39.8 us (12%)
  blocking collectives  27.5 us (8%)
  other arithmetic  22.3 us (7%)
  between operations  13.5 us (4%)
  matrix products  9.52 us (3%)
    all_to_all x1, waiting for transfers between devices, regroup(): blocks = lax.all_to_all(blocks, 'dp', split_axis=0, concat_axis=0)  50.7 us
    all_to_all x2, waiting for transfers between devices, exchange_in_pieces(): lax.all_to_all(piece, axis, split_axis=0, concat_axis=0, tiled=True)  50.6 us
    convert_element_type x3, local copies, waits for them, and re-layouts, shards(): arrived.astype(jnp.float32)  44.7 us
    all_gather x1, waiting for transfers between devices, turned_gather(): whole = lax.all_gather(both, axis, axis=0, tiled=True)  40.9 us
    all_to_all x1, blocking collectives, regroup(): lax.all_to_all(weight_slab, 'dp', split_axis=2, concat_axis=3, tiled=True)  27.5 us
    all_to_all x2, starting transfers between devices, exchange_in_pieces(): lax.all_to_all(piece, axis, split_axis=0, concat_axis=0, tiled=True)  20.4 us
    all_to_all x1, waiting for transfers between devices, copy_for_each(): return lax.all_to_all(copies, axis, split_axis=0, concat_axis=0, tiled=True)  12.4 us
    convert_element_type x1, other arithmetic, shards(): return (merged * scaling[:, :, :, None]).astype(jnp.bfloat16)  10.6 us
  transfers between devices with their start and end apart: 5, of which 5 were waited for; matrix products, arithmetic and copies ran while one was open for 4% of the time, Pallas kernels for 0%

profile of v1, /device:TPU:1, one launch (start us, length us, event | category | flops | bytes accessed | tf_op | source)
XLA Modules:
  0.0 340.8 jit_solution(7267961644394016183)
XLA Ops:
  6.5 3.4 copy.19
  9.9 27.5 %all_to_all.35 = bf16[2,2,64,3584]{3,1,0,2:T(2,128)(2,1)S(1)} all-to-all(bf16[2,2,64,3584]{3,1,0,2:T(2,128)(2,1)S(1)} %copy.19), channel_id=1, replica_groups=mesh['tensor'=64,'dp'=4] {'dp'}, dimensions={2} | all-to-all | bytes 3670016 | tf_op jit(solution)/shard_map/all_to_all | solution.py:64
  37.4 2.6 copy.30
  40.1 4.4 %reshape.28 = bf16[2,2,16,64,224]{4,3,2,1,0:T(8,128)(2,1)S(1)} reshape(bf16[2,2,16,4,3584]{4,3,2,1,0:T(4,128)(2,1)} %bitcast.46) | data formatting | bytes 3670016 | tf_op jit(solution)/shard_map/reshape | solution.py:9
  44.6 1.6 copy.22
  46.2 12.6 %all-to-all-start.2 = ((bf16[64,2,2,8,224]{4,3,2,1,0:T(8,128)(2,1)}), bf16[64,2,2,8,224]{4,3,2,1,0:T(8,128)(2,1)S(1)}, u32[]{:S(2)}, u32[]{:S(2)}) async-start(bf16[64,2,2,8,224]{4,3,2,1,0:T(8,128)(2,1)} %copy.22), calls=%async_computation.2 | async-start | bytes 2097152 | tf_op jit(solution)/shard_map/all_to_all | solution.py:31
  58.8 1.6 copy.21
  60.4 26.0 %all-to-all-done.2 = bf16[64,2,2,8,224]{4,3,2,1,0:T(8,128)(2,1)S(1)} async-done(((bf16[64,2,2,8,224]{4,3,2,1,0:T(8,128)(2,1)}), bf16[64,2,2,8,224]{4,3,2,1,0:T(8,128)(2,1)S(1)}, u32[]{:S(2)}, u32[]{:S(2)}) %all-to-all-start.2) | async-done | bytes 917536 | tf_op jit(solution)/shard_map/all_to_all | solution.py:31
  86.4 7.8 %all-to-all-start.1 = ((bf16[64,2,2,8,224]{4,3,2,1,0:T(8,128)(2,1)}), bf16[64,2,2,8,224]{4,3,2,1,0:T(8,128)(2,1)S(1)}, u32[]{:S(2)}, u32[]{:S(2)}) async-start(bf16[64,2,2,8,224]{4,3,2,1,0:T(8,128)(2,1)} %copy.21), calls=%async_computation.1 | async-start | bytes 2097152 | tf_op jit(solution)/shard_map/all_to_all | solution.py:31
  94.2 0.2 broadcast_bitcast_fusion
  94.5 1.5 reshape.36
  96.0 24.6 %all-to-all-done.1 = bf16[64,2,2,8,224]{4,3,2,1,0:T(8,128)(2,1)S(1)} async-done(((bf16[64,2,2,8,224]{4,3,2,1,0:T(8,128)(2,1)}), bf16[64,2,2,8,224]{4,3,2,1,0:T(8,128)(2,1)S(1)}, u32[]{:S(2)}, u32[]{:S(2)}) %all-to-all-start.1) | async-done | bytes 917536 | tf_op jit(solution)/shard_map/all_to_all | solution.py:31
  120.6 8.9 %all-to-all-start.4 = ((bf16[64,2,2048]{2,1,0:T(2,128)(2,1)}), bf16[64,2,2048]{2,1,0:T(2,128)(2,1)}, u32[]{:S(2)}, u32[]{:S(2)}) async-start(bf16[64,2,2048]{2,1,0:T(2,128)(2,1)} %reshape.36), calls=%async_computation.4 | async-start | bytes 1048576 | tf_op jit(solution)/shard_map/all_to_all | solution.py:37
  129.5 0.6 maximum_bitcast_fusion
  130.2 0.2 copy.23
  130.4 2.4 copy.24
  132.8 12.4 %all-to-all-done.4 = bf16[64,2,2048]{2,1,0:T(2,128)(2,1)} async-done(((bf16[64,2,2048]{2,1,0:T(2,128)(2,1)}), bf16[64,2,2048]{2,1,0:T(2,128)(2,1)}, u32[]{:S(2)}, u32[]{:S(2)}) %all-to-all-start.4) | async-done | bytes 524320 | tf_op jit(solution)/shard_map/all_to_all | solution.py:37
  145.2 5.5 %stack.3 = bf16[4,2,2,1024,224]{3,4,2,1,0:T(8,128)(2,1)} broadcast(bf16[2,2,1024,224]{2,3,1,0:T(8,128)(2,1)} %copy.24), dimensions={1,2,3,4} | broadcast | bytes 9175040 | tf_op jit(solution)/shard_map/stack | solution.py:67
  150.8 10.5 %all-to-all-start.3 = ((bf16[4,2,2,1024,224]{3,4,2,1,0:T(8,128)(2,1)}), bf16[4,2,2,1024,224]{3,4,2,1,0:T(8,128)(2,1)}, u32[]{:S(2)}, u32[]{:S(2)}) async-start(bf16[4,2,2,1024,224]{3,4,2,1,0:T(8,128)(2,1)} %stack.3), calls=%async_computation.3 | async-start | bytes 14680064 | tf_op jit(solution)/shard_map/all_to_all | solution.py:68
  161.4 0.9 pad_maximum_fusion
  162.3 2.3 reshape.37
  164.7 0.7 copy.27
  165.4 0.8 reshape.32
  166.2 40.9 %all-gather.2.cloned.1.call-done = bf16[14336,68]{0,1:T(8,128)(2,1)} async-done(((bf16[3584,68]{0,1:T(8,128)(2,1)}), bf16[14336,68]{0,1:T(8,128)(2,1)}) %all-gather.2.cloned.1.call-update) | async-done | bytes 1949712 | tf_op jit(solution)/shard_map/all_gather | solution.py:49
  207.1 1.0 split.19
  208.2 50.7 %all-to-all-done.3 = bf16[4,2,2,1024,224]{3,4,2,1,0:T(8,128)(2,1)} async-done(((bf16[4,2,2,1024,224]{3,4,2,1,0:T(8,128)(2,1)}), bf16[4,2,2,1024,224]{3,4,2,1,0:T(8,128)(2,1)}, u32[]{:S(2)}, u32[]{:S(2)}) %all-to-all-start.3) | async-done | bytes 7340064 | tf_op jit(solution)/shard_map/all_to_all | solution.py:68
  258.9 10.2 %convert_bitcast_fusion = f32[2,2,4,1024,224]{3,4,1,0,2:T(8,128)} fusion(bf16[4,2,2,1024,224]{3,4,2,1,0:T(8,128)(2,1)} %all-to-all-done.3), kind=kLoop, calls=%fused_computation | loop fusion | flops 3670016 | bytes 22020096 | tf_op jit(solution)/shard_map/convert_element_type | solution.py:89
  269.1 15.8 %copy.25 = f32[2,2,4,1024,224]{4,3,2,1,0:T(8,128)} copy(f32[2,2,4,1024,224]{3,4,1,0,2:T(8,128)} %convert_bitcast_fusion) | data formatting | bytes 29360128 | tf_op jit(solution)/shard_map/convert_element_type | solution.py:89
  284.8 11.9 %copy.26 = f32[2,2,224,64,4,16]{2,5,4,3,1,0:T(8,128)} copy(f32[2,2,224,64,4,16]{2,5,3,4,1,0:T(8,128)} %bitcast.41) | data formatting | bytes 29360128 | tf_op jit(solution)/shard_map/convert_element_type | solution.py:89
  296.8 17.0 %copy.28 = f32[2,2,224,4096]{3,2,1,0:T(8,128)} copy(f32[2,2,224,4096]{2,3,1,0:T(8,128)} %bitcast.42) | data formatting | bytes 29360128 | tf_op jit(solution)/shard_map/convert_element_type | solution.py:89
  313.8 9.5 %multiply_reduce_fusion = (f32[2,2,224]{2,1,0:T(2,128)S(1)}, f32[2,2,224,4096]{3,2,1,0:T(8,128)}) fusion(f32[2,2,224,4096]{3,2,1,0:T(8,128)} %copy.28, bf16[2,2,4096,16]{2,3,1,0:T(8,128)(2,1)S(1)} %reshape.32, bf16[14336,2,2,16]{0,3,2,1:T(8,128)(2,1)S(1)} %bitcast.47, s32[]{:T(128)S(6)} %select_n.4), kind=kOutput, calls=%fused_computation.2 | convolution fusion | flops 128449664 | bytes 29920772 | tf_op jit(solution)/shard_map/xyrf,xyir->xyfi/dot_general | solution.py:89
  323.4 10.6 %multiply_convert_fusion = bf16[2,2,224,4096]{3,2,1,0:T(8,128)(2,1)} fusion(f32[2,2,224,4096]{3,2,1,0:T(8,128)} %get-tuple-element.8, f32[2,2,224]{2,1,0:T(2,128)S(1)} %bitcast_multiply_fusion), kind=kLoop, calls=%fused_computation.1 | loop fusion | flops 7340032 | bytes 22023680 | tf_op jit(solution)/shard_map/convert_element_type | solution.py:94
  (17 shorter events, 0.5 us)
Async XLA Ops:
  6.5 87.7 %copy-start = (bf16[2,2,64,16]{2,3,1,0:T(8,128)(2,1)S(1)}, bf16[2,2,64,16]{2,3,1,0:T(8,128)(2,1)}, u32[]{:S(2)}) copy-start(bf16[2,2,64,16]{2,3,1,0:T(8,128)(2,1)} %param.5) | copy-start | bytes 24580
  46.2 40.2 %all-to-all-start.2 = ((bf16[64,2,2,8,224]{4,3,2,1,0:T(8,128)(2,1)}), bf16[64,2,2,8,224]{4,3,2,1,0:T(8,128)(2,1)S(1)}, u32[]{:S(2)}, u32[]{:S(2)}) async-start(bf16[64,2,2,8,224]{4,3,2,1,0:T(8,128)(2,1)} %copy.22), calls=%async_computation.2 | async-start | bytes 2097152 | tf_op jit(solution)/shard_map/all_to_all | solution.py:31
  86.4 34.3 %all-to-all-start.1 = ((bf16[64,2,2,8,224]{4,3,2,1,0:T(8,128)(2,1)}), bf16[64,2,2,8,224]{4,3,2,1,0:T(8,128)(2,1)S(1)}, u32[]{:S(2)}, u32[]{:S(2)}) async-start(bf16[64,2,2,8,224]{4,3,2,1,0:T(8,128)(2,1)} %copy.21), calls=%async_computation.1 | async-start | bytes 2097152 | tf_op jit(solution)/shard_map/all_to_all | solution.py:31
  120.6 24.6 %all-to-all-start.4 = ((bf16[64,2,2048]{2,1,0:T(2,128)(2,1)}), bf16[64,2,2048]{2,1,0:T(2,128)(2,1)}, u32[]{:S(2)}, u32[]{:S(2)}) async-start(bf16[64,2,2048]{2,1,0:T(2,128)(2,1)} %reshape.36), calls=%async_computation.4 | async-start | bytes 1048576 | tf_op jit(solution)/shard_map/all_to_all | solution.py:37
  150.8 10.6 %copy-start.3 = (bf16[2,2,3584]{2,1,0:T(2,128)(2,1)S(1)}, bf16[2,2,3584]{2,1,0:T(2,128)(2,1)}, u32[]{:S(2)}) copy-start(bf16[2,2,3584]{2,1,0:T(2,128)(2,1)} %param.7) | copy-start | bytes 86020
  150.8 10.6 %copy-start.2 = (bf16[2,2,16,3584]{3,2,1,0:T(8,128)(2,1)S(1)}, bf16[2,2,16,3584]{3,2,1,0:T(8,128)(2,1)}, u32[]{:S(2)}) copy-start(bf16[2,2,16,3584]{3,2,1,0:T(8,128)(2,1)} %param.6) | copy-start | bytes 1376260
  150.8 108.1 %all-to-all-start.3 = ((bf16[4,2,2,1024,224]{3,4,2,1,0:T(8,128)(2,1)}), bf16[4,2,2,1024,224]{3,4,2,1,0:T(8,128)(2,1)}, u32[]{:S(2)}, u32[]{:S(2)}) async-start(bf16[4,2,2,1024,224]{3,4,2,1,0:T(8,128)(2,1)} %stack.3), calls=%async_computation.3 | async-start | bytes 14680064 | tf_op jit(solution)/shard_map/all_to_all | solution.py:68
  161.3 45.8 %all-gather.2.cloned.1.call-start = ((), (), s32[]{:S(2)}) async-start(), calls=%async_computation.5 | async-start | bytes 2580480 | tf_op jit(solution)/shard_map/all_gather | solution.py:49
  296.8 17.0 %slice-start = ((bf16[14336,68]{0,1:T(8,128)(2,1)}), bf16[14336,64]{0,1:T(8,128)(2,1)S(1)}, s32[]{:S(2)}) async-start(bf16[14336,68]{0,1:T(8,128)(2,1)} %all-gather.2.cloned.1.call-done), calls=%async_computation.6 | async-start | bytes 3670016 | tf_op jit(solution)/shard_map/split | solution.py:50
  323.4 10.6 %copy-start.1 = (bf16[2,2,64,16]{2,3,1,0:T(8,128)(2,1)S(1)}, bf16[2,2,64,16]{2,3,1,0:T(8,128)(2,1)}, u32[]{:S(2)}) copy-start(bf16[2,2,64,16]{2,3,1,0:T(8,128)(2,1)} %param.5) | copy-start | bytes 24580
Sparse Core Ops, SparseCore 0:
  163.9 43.1 all-gather.1
